TPU v7x, 32 devices: a whole 2x2x4 slice. The times are simulated.
32 devices in a mesh: fsdp: 2 (over y), trow: 4 (over x, core), tcol: 4 (over z).
Axes of the slice: x: 2, y: 2, z: 4, core: 2. Of those that a mesh axis runs over, the one named last changes fastest.
Arguments:
- tokens: bfloat16 [512, 4096], P('fsdp', 'tcol'), may hold values from -100 to 100
- w_up: bfloat16 [4096, 16384], P('tcol', ('fsdp', 'trow')), may hold values from -0.1875 to 0.1875
- w_down: bfloat16 [16384, 4096], P(('fsdp', 'trow'), 'tcol'), may hold values from -0.046875 to 0.046875
- cotangent: bfloat16 [512, 4096], P('fsdp', 'tcol'), may hold values from -6 to 6
Outputs:
- mixed: bfloat16 [512, 4096], P('fsdp', 'tcol')
- input_gradient: bfloat16 [512, 4096], P('fsdp', 'tcol')
- grad_up: bfloat16 [4096, 16384], P('tcol', ('fsdp', 'trow'))
- grad_down: bfloat16 [16384, 4096], P(('fsdp', 'trow'), 'tcol')
All inputs are finite; a program needn't handle non-finite values.
Results may differ from a plain program's by a relative error of at most 0.02.
Values may be sent and summed in bfloat16 or wider, within the bound.
A program may use at most 128 MiB of HBM per device.

v0:
```python
import jax
import jax.numpy as jnp
from jax import lax
from jax.sharding import PartitionSpec as P


def gelu_value(pre):
    phi = 0.5 * (1.0 + jax.scipy.special.erf(pre * 0.7071067811865476))
    return pre * phi


def gelu_slope(pre):
    phi = 0.5 * (1.0 + jax.scipy.special.erf(pre * 0.7071067811865476))
    return phi + pre * jnp.exp(-0.5 * pre * pre) * 0.3989422804014327


def contract(left, right, left_dim, right_dim):
    return lax.dot_general(
        left, right, (((left_dim,), (right_dim,)), ((), ())), preferred_element_type=jnp.float32
    )


def local(tokens, w_up, w_down, cotangent):
    width = tokens.shape[1] * lax.axis_size("tcol")
    input_float = tokens.astype(jnp.float32)
    cot_all = lax.all_gather(cotangent, "fsdp", axis=0, tiled=True)
    sum_one, sum_two = lax.psum(
        (jnp.sum(input_float, axis=1), jnp.sum(input_float * input_float, axis=1)), "tcol"
    )
    token_mean = sum_one / width
    var = sum_two / width - token_mean * token_mean
    inverse_stddev = lax.rsqrt(var + 1e-05)
    centered_scaled = (input_float - token_mean[:, None]) * inverse_stddev[:, None]
    normalized_rows = centered_scaled.astype(jnp.bfloat16)
    normed_all = lax.all_gather(normalized_rows, "fsdp", axis=0, tiled=True)
    dhid_part = contract(cot_all, w_down, 1, 1).astype(jnp.bfloat16)
    dhid = lax.psum_scatter(dhid_part, "tcol", scatter_dimension=0, tiled=True).astype(jnp.float32)
    pre_part = contract(normed_all, w_up, 1, 0).astype(jnp.bfloat16)
    pre = lax.psum_scatter(pre_part, "tcol", scatter_dimension=0, tiled=True).astype(jnp.float32)
    hidden = lax.all_gather(gelu_value(pre).astype(jnp.bfloat16), "tcol", axis=0, tiled=True)
    dpre = lax.all_gather((dhid * gelu_slope(pre)).astype(jnp.bfloat16), "tcol", axis=0, tiled=True)
    branch_part = contract(hidden, w_down, 1, 0).astype(jnp.bfloat16)
    branch = lax.psum_scatter(branch_part, "fsdp", scatter_dimension=0, tiled=True)
    branch = lax.psum(branch, "trow").astype(jnp.float32)
    mixed = (input_float + branch).astype(jnp.bfloat16)
    grad_down = contract(hidden, cot_all, 0, 0).astype(jnp.bfloat16)
    dnorm_part = contract(dpre, w_up, 1, 1).astype(jnp.bfloat16)
    dnorm = lax.psum_scatter(dnorm_part, "fsdp", scatter_dimension=0, tiled=True)
    normed_gradient = lax.psum(dnorm, "trow").astype(jnp.float32)
    grad_up = contract(normed_all, dpre, 0, 0).astype(jnp.bfloat16)
    mean_first, mean_second = lax.psum(
        (jnp.sum(normed_gradient, axis=1), jnp.sum(normed_gradient * centered_scaled, axis=1)),
        "tcol",
    )
    first_moment = mean_first / width
    second_moment = mean_second / width
    input_gradient = cotangent.astype(jnp.float32) + inverse_stddev[:, None] * (
        normed_gradient - first_moment[:, None] - centered_scaled * second_moment[:, None]
    )
    return (mixed, input_gradient.astype(jnp.bfloat16), grad_up, grad_down)


def solution(mesh):
    return jax.shard_map(
        local,
        mesh=mesh,
        in_specs=(
            P("fsdp", "tcol"),
            P("tcol", ("fsdp", "trow")),
            P(("fsdp", "trow"), "tcol"),
            P("fsdp", "tcol"),
        ),
        out_specs=(
            P("fsdp", "tcol"),
            P("fsdp", "tcol"),
            P("tcol", ("fsdp", "trow")),
            P(("fsdp", "trow"), "tcol"),
        ),
        check_vma=False,
    )
```

profile of v0, /device:TPU:0, one launch (start us, length us, event | category | flops | bytes accessed | tf_op | source)
XLA Modules:
  0.0 359.4 jit_solution(15157938787356180238)
XLA Ops:
  7.2 0.0 all-gather.5.cloned.1.call-start
  7.2 1.3 convert_reduce_fusion
  8.5 13.5 %all-reduce.1 = (f32[256]{0:T(256)S(1)}, f32[256]{0:T(256)S(1)}) all-reduce(f32[256]{0:T(256)S(1)} %get-tuple-element.7, f32[256]{0:T(256)S(1)} %get-tuple-element.6), channel_id=1, replica_groups=mesh['fsdp'=2,'trow'=4,'tcol'=4] {'tcol'}, use_global_device_ids=true, to_apply=%region_3.0 | all-reduce | flops 512 | bytes 4096 | tf_op jit(solution)/shard_map/psum | solution.py:27
  22.0 2.1 fusion.7
  24.1 0.0 all-gather.5.cloned.1.call-update
  24.1 0.0 all-gather.9.cloned.1.call-start
  24.2 0.7 all-gather.9.cloned.1.call-update
  24.9 0.0 reduce-scatter.5.cloned.1.call-start
  24.9 18.9 %all-gather.5.cloned.1.call-done = bf16[512,1024]{1,0:T(8,128)(2,1)} async-done(((bf16[256,1024]{1,0:T(8,128)(2,1)}), bf16[512,1024]{1,0:T(8,128)(2,1)}) %all-gather.5.cloned.1.call-update) | async-done | bytes 1048592 | tf_op jit(solution)/shard_map/all_gather | solution.py:35
  43.8 6.2 %convolution_convert_fusion.3 = bf16[512,2048]{1,0:T(8,128)(2,1)} fusion(bf16[512,1024]{1,0:T(8,128)(2,1)} %all-gather.5.cloned.1.call-done, bf16[1024,2048]{1,0:T(8,128)(2,1)} %param.5), kind=kOutput, calls=%fused_computation.3 | convolution fusion | flops 2148532224 | bytes 7340032 | tf_op jit(solution)/shard_map/dot_general | solution.py:18
  49.9 0.0 reduce-scatter.5.cloned.1.call-update
  49.9 0.0 reduce-scatter.9.cloned.1.call-start
  50.0 16.6 %all-gather.9.cloned.1.call-done = bf16[512,1024]{1,0:T(8,128)(2,1)} async-done(((bf16[256,1024]{1,0:T(8,128)(2,1)}), bf16[512,1024]{1,0:T(8,128)(2,1)}) %all-gather.9.cloned.1.call-update) | async-done | bytes 1048592 | tf_op jit(solution)/shard_map/all_gather | solution.py:26
  66.6 6.2 %convolution_convert_fusion.2 = bf16[512,2048]{1,0:T(8,128)(2,1)} fusion(bf16[512,1024]{1,0:T(8,128)(2,1)} %all-gather.9.cloned.1.call-done, bf16[2048,1024]{1,0:T(8,128)(2,1)} %param.6), kind=kOutput, calls=%fused_computation.2 | convolution fusion | flops 2148532224 | bytes 7340032 | tf_op jit(solution)/shard_map/dot_general | solution.py:18
  72.8 0.0 reduce-scatter.9.cloned.1.call-update
  72.8 0.0 all-gather.7.cloned.1.call-start
  72.9 40.3 %reduce-scatter.5.cloned.1.call-done = bf16[128,2048]{1,0:T(8,128)(2,1)} async-done(((bf16[512,2048]{1,0:T(8,128)(2,1)}), bf16[128,2048]{1,0:T(8,128)(2,1)}) %reduce-scatter.5.cloned.1.call-update) | async-done | bytes 524304 | tf_op jit(solution)/shard_map/reduce_scatter | solution.py:39
  113.2 45.6 %reduce-scatter.9.cloned.1.call-done = bf16[128,2048]{1,0:T(8,128)(2,1)} async-done(((bf16[512,2048]{1,0:T(8,128)(2,1)}), bf16[128,2048]{1,0:T(8,128)(2,1)}) %reduce-scatter.9.cloned.1.call-update) | async-done | bytes 524304 | tf_op jit(solution)/shard_map/reduce_scatter | solution.py:37
  158.7 2.7 fusion.18
  161.4 0.0 all-gather.7.cloned.1.call-update
  161.5 0.0 all-gather.11.cloned.1.call-start
  161.5 0.5 all-gather.11.cloned.1.call-update
  162.0 0.0 reduce-scatter.7.cloned.1.call-start
  162.1 44.4 %all-gather.7.cloned.1.call-done = bf16[512,2048]{1,0:T(8,128)(2,1)} async-done(((bf16[128,2048]{1,0:T(8,128)(2,1)}), bf16[512,2048]{1,0:T(8,128)(2,1)}) %all-gather.7.cloned.1.call-update) | async-done | bytes 2097168 | tf_op jit(solution)/shard_map/all_gather | solution.py:40
  206.5 6.1 %convolution_convert_fusion.5 = bf16[512,1024]{1,0:T(8,128)(2,1)} fusion(bf16[512,2048]{1,0:T(8,128)(2,1)} %all-gather.7.cloned.1.call-done, bf16[2048,1024]{1,0:T(8,128)(2,1)} %param.6), kind=kOutput, calls=%fused_computation.17 | convolution fusion | flops 2148007936 | bytes 7340032 | tf_op jit(solution)/shard_map/dot_general | solution.py:18
  212.6 0.0 reduce-scatter.7.cloned.1.call-update
  212.6 0.0 copy-start.2
  212.6 0.0 copy-start.5
  212.6 0.0 reduce-scatter.11.cloned.1.call-start
  212.7 40.3 %all-gather.11.cloned.1.call-done = bf16[512,2048]{1,0:T(8,128)(2,1)} async-done(((bf16[128,2048]{1,0:T(8,128)(2,1)}), bf16[512,2048]{1,0:T(8,128)(2,1)}) %all-gather.11.cloned.1.call-update) | async-done | bytes 2097168 | tf_op jit(solution)/shard_map/all_gather | solution.py:41
  253.0 6.2 %convolution_convert_fusion.4 = bf16[512,1024]{1,0:T(8,128)(2,1)} fusion(bf16[512,2048]{1,0:T(8,128)(2,1)} %all-gather.11.cloned.1.call-done, bf16[1024,2048]{1,0:T(8,128)(2,1)} %param.5), kind=kOutput, calls=%fused_computation.16 | convolution fusion | flops 2148007936 | bytes 7340032 | tf_op jit(solution)/shard_map/dot_general | solution.py:18
  259.1 0.0 reduce-scatter.11.cloned.1.call-update
  259.1 0.2 all-reduce.5.cloned.1.call-start
  259.4 15.6 %reduce-scatter.7.cloned.1.call-done = bf16[256,1024]{1,0:T(8,128)(2,1)} async-done(((bf16[512,1024]{1,0:T(8,128)(2,1)}), bf16[256,1024]{1,0:T(8,128)(2,1)}) %reduce-scatter.7.cloned.1.call-update) | async-done | bytes 524304 | tf_op jit(solution)/shard_map/reduce_scatter | solution.py:43
  275.0 23.2 %reduce-scatter.11.cloned.1.call-done = bf16[256,1024]{1,0:T(8,128)(2,1)} async-done(((bf16[512,1024]{1,0:T(8,128)(2,1)}), bf16[256,1024]{1,0:T(8,128)(2,1)}) %reduce-scatter.11.cloned.1.call-update) | async-done | bytes 524304 | tf_op jit(solution)/shard_map/reduce_scatter | solution.py:48
  298.2 0.0 all-reduce.5.cloned.1.call-update
  298.3 0.0 copy-done.2
  298.3 0.0 copy-done.5
  298.3 0.0 copy-start.3
  298.3 0.0 copy-start.4
  298.3 4.4 %convolution_convert_fusion = bf16[2048,1024]{1,0:T(8,128)(2,1)} fusion(bf16[512,2048]{1,0:T(8,128)(2,1)S(1)} %copy-done.2, bf16[512,1024]{1,0:T(8,128)(2,1)S(1)} %copy-done.5), kind=kOutput, calls=%fused_computation | convolution fusion | flops 2149580800 | bytes 7340032 | tf_op jit(solution)/shard_map/dot_general | solution.py:18
  302.7 0.0 copy-done.3
  302.7 0.0 copy-done.4
  302.7 0.0 copy-start
  302.7 0.0 copy-start.1
  302.7 4.4 %convolution_convert_fusion.1 = bf16[1024,2048]{1,0:T(8,128)(2,1)} fusion(bf16[512,1024]{1,0:T(8,128)(2,1)S(1)} %copy-done.4, bf16[512,2048]{1,0:T(8,128)(2,1)S(1)} %copy-done.3), kind=kOutput, calls=%fused_computation.1 | convolution fusion | flops 2149580800 | bytes 7340032 | tf_op jit(solution)/shard_map/dot_general | solution.py:18
  307.2 29.9 %all-reduce.5.cloned.1.call-done = (bf16[256,1024]{1,0:T(8,128)(2,1)}, bf16[256,1024]{1,0:T(8,128)(2,1)}) async-done(((bf16[256,1024]{1,0:T(8,128)(2,1)}, bf16[256,1024]{1,0:T(8,128)(2,1)}), (bf16[256,1024]{1,0:T(8,128)(2,1)}, bf16[256,1024]{1,0:T(8,128)(2,1)})) %all-reduce.5.cloned.1.call-update) | async-done | bytes 1048592 | tf_op jit(solution)/shard_map/psum | solution.py:44
  337.1 0.0 copy-done
  337.1 1.5 convert_reduce_fusion.1
  338.5 11.7 %all-reduce = (f32[256]{0:T(256)S(1)}, f32[256]{0:T(256)S(1)}) all-reduce(f32[256]{0:T(256)S(1)} %get-tuple-element.5, f32[256]{0:T(256)S(1)} %get-tuple-element.4), channel_id=1, replica_groups=mesh['fsdp'=2,'trow'=4,'tcol'=4] {'tcol'}, use_global_device_ids=true, to_apply=%region_13.0 | all-reduce | flops 512 | bytes 4096 | tf_op jit(solution)/shard_map/psum | solution.py:51
  350.2 0.0 copy-done.1
  350.2 2.6 fusion.3
  (2 shorter events, 0.0 us)
Async XLA Ops:
  7.2 36.6 %all-gather.5.cloned.1.call-start = ((), (), s32[]{:S(2)}) async-start(), calls=%async_computation.4 | async-start | bytes 1572864 | tf_op jit(solution)/shard_map/all_gather | solution.py:35
  24.1 42.5 %all-gather.9.cloned.1.call-start = ((), (), s32[]{:S(2)}) async-start(), calls=%async_computation.8 | async-start | bytes 1572864 | tf_op jit(solution)/shard_map/all_gather | solution.py:26
  24.9 88.3 %reduce-scatter.5.cloned.1.call-start = ((), (), s32[]{:S(2)}) async-start(), calls=%async_computation.5 | async-start | bytes 2621440 | tf_op jit(solution)/shard_map/reduce_scatter | solution.py:39
  49.9 108.8 %reduce-scatter.9.cloned.1.call-start = ((), (), s32[]{:S(2)}) async-start(), calls=%async_computation.9 | async-start | bytes 2621440 | tf_op jit(solution)/shard_map/reduce_scatter | solution.py:37
  72.8 133.6 %all-gather.7.cloned.1.call-start = ((), (), s32[]{:S(2)}) async-start(), calls=%async_computation.6 | async-start | bytes 2621440 | tf_op jit(solution)/shard_map/all_gather | solution.py:40
  161.5 91.5 %all-gather.11.cloned.1.call-start = ((), (), s32[]{:S(2)}) async-start(), calls=%async_computation.10 | async-start | bytes 2621440 | tf_op jit(solution)/shard_map/all_gather | solution.py:41
  162.0 113.0 %reduce-scatter.7.cloned.1.call-start = ((), (), s32[]{:S(2)}) async-start(), calls=%async_computation.7 | async-start | bytes 1572864 | tf_op jit(solution)/shard_map/reduce_scatter | solution.py:43
  212.6 85.6 %copy-start.2 = (bf16[512,2048]{1,0:T(8,128)(2,1)S(1)}, bf16[512,2048]{1,0:T(8,128)(2,1)}, u32[]{:S(2)}) copy-start(bf16[512,2048]{1,0:T(8,128)(2,1)} %all-gather.7.cloned.1.call-done) | copy-start | bytes 6291460
  212.6 85.6 %copy-start.5 = (bf16[512,1024]{1,0:T(8,128)(2,1)S(1)}, bf16[512,1024]{1,0:T(8,128)(2,1)}, u32[]{:S(2)}) copy-start(bf16[512,1024]{1,0:T(8,128)(2,1)} %all-gather.9.cloned.1.call-done) | copy-start | bytes 3145732
  212.6 85.6 %reduce-scatter.11.cloned.1.call-start = ((), (), s32[]{:S(2)}) async-start(), calls=%async_computation.11 | async-start | bytes 1572864 | tf_op jit(solution)/shard_map/reduce_scatter | solution.py:48
  259.1 77.9 %all-reduce.5.cloned.1.call-start = ((), (), s32[]{:S(2)}) async-start(), calls=%async_computation.12 | async-start | bytes 2097152 | tf_op jit(solution)/shard_map/psum | solution.py:44
  298.3 4.4 %copy-start.3 = (bf16[512,2048]{1,0:T(8,128)(2,1)S(1)}, bf16[512,2048]{1,0:T(8,128)(2,1)}, u32[]{:S(2)}) copy-start(bf16[512,2048]{1,0:T(8,128)(2,1)} %all-gather.11.cloned.1.call-done) | copy-start | bytes 6291460
  298.3 4.4 %copy-start.4 = (bf16[512,1024]{1,0:T(8,128)(2,1)S(1)}, bf16[512,1024]{1,0:T(8,128)(2,1)}, u32[]{:S(2)}) copy-start(bf16[512,1024]{1,0:T(8,128)(2,1)} %all-gather.5.cloned.1.call-done) | copy-start | bytes 3145732
  302.7 34.3 %copy-start = (bf16[256,1024]{1,0:T(8,128)(2,1)S(1)}, bf16[256,1024]{1,0:T(8,128)(2,1)}, u32[]{:S(2)}) copy-start(bf16[256,1024]{1,0:T(8,128)(2,1)} %param.4) | copy-start | bytes 1572868
  302.7 47.5 %copy-start.1 = (bf16[256,1024]{1,0:T(8,128)(2,1)S(1)}, bf16[256,1024]{1,0:T(8,128)(2,1)}, u32[]{:S(2)}) copy-start(bf16[256,1024]{1,0:T(8,128)(2,1)} %param.7) | copy-start | bytes 1572868
Sparse Core Ops, SparseCore 0:
  24.2 19.4 all-gather.4
  45.3 21.2 all-gather.8
  69.5 43.6 reduce-scatter.4
  115.9 42.8 reduce-scatter.8
  161.6 44.8 all-gather.6
  208.5 44.4 all-gather.10
  255.8 19.1 reduce-scatter.6
  277.8 20.3 reduce-scatter.10
  300.7 36.3 all-reduce.4
where the time goes:
time: 360 us; the launch traced here: 359 us
  waiting for transfers between devices  276 us (77%)
  matrix products  33.5 us (9%)
  blocking collectives  25.2 us (7%)
  between operations  13.9 us (4%)
  other arithmetic  10.2 us (3%)
    reduce_scatter x1, waiting for transfers between devices, local(): lax.psum_scatter(dhid_part, 'tcol', scatter_dimension=0, tiled=True)  45.6 us
    all_gather x1, waiting for transfers between devices, local(): lax.all_gather(gelu_value(pre).astype(jnp.bfloat16), 'tcol', axis=0, tile...  44.4 us
    all_gather x1, waiting for transfers between devices, local(): lax.all_gather((dhid * gelu_slope(pre)).astype(jnp.bfloat16), 'tcol', axi...  40.3 us
    reduce_scatter x1, waiting for transfers between devices, local(): lax.psum_scatter(pre_part, 'tcol', scatter_dimension=0, tiled=True)  40.3 us
    dot_general x6, matrix products, contract(): lax.dot_general(left, right, (((left_dim,), (right_dim,)), ((), ())), pre...  33.5 us
    psum x1, waiting for transfers between devices, local(): branch = lax.psum(branch, 'trow').astype(jnp.float32)  29.9 us
    reduce_scatter x1, waiting for transfers between devices, local(): lax.psum_scatter(dnorm_part, 'fsdp', scatter_dimension=0, tiled=True)  23.2 us
    all_gather x1, waiting for transfers between devices, local(): normed_all = lax.all_gather(normalized_rows, 'fsdp', axis=0, tiled=True)  18.9 us
  transfers between devices with their start and end apart: 9, of which 9 were waited for; matrix products, arithmetic and copies ran while one was open for 9% of the time, Pallas kernels for 0%

commit v1 on v0

--- a/solution.py
+++ b/solution.py
@@ -2,6 +2,12 @@
 import jax.numpy as jnp
 from jax import lax
 from jax.sharding import PartitionSpec as P
+
+
+def in_order(pieces, dim):
+    shape = list(pieces.shape[1:])
+    shape[dim] *= pieces.shape[0]
+    return jnp.moveaxis(pieces, 0, dim).reshape(shape)
 
 
 def gelu_value(pre):
@@ -38,7 +44,20 @@
     pre_part = contract(normed_all, w_up, 1, 0).astype(jnp.bfloat16)
     pre = lax.psum_scatter(pre_part, "tcol", scatter_dimension=0, tiled=True).astype(jnp.float32)
     hidden = lax.all_gather(gelu_value(pre).astype(jnp.bfloat16), "tcol", axis=0, tiled=True)
-    dpre = lax.all_gather((dhid * gelu_slope(pre)).astype(jnp.bfloat16), "tcol", axis=0, tiled=True)
+    x = (dhid * gelu_slope(pre)).astype(jnp.bfloat16)
+    devices = lax.axis_size("tcol")
+    pairs = [(i, (i + 1) % devices) for i in range(devices)]
+    back = [(b, a) for a, b in pairs]
+    lower, upper = ([], [])
+    for step in range(devices - 1):
+        if step % 2 == 0:
+            lower.append(lax.ppermute(lower[-1] if lower else x, "tcol", pairs))
+        else:
+            upper.append(lax.ppermute(upper[-1] if upper else x, "tcol", back))
+    blocks = jnp.stack([*lower[::-1], x, *upper])
+    shift = lax.axis_index("tcol") - len(lower)
+    blocks = blocks[(jnp.arange(devices) - shift) % devices]
+    dpre = in_order(blocks, 0)
     branch_part = contract(hidden, w_down, 1, 0).astype(jnp.bfloat16)
     branch = lax.psum_scatter(branch_part, "fsdp", scatter_dimension=0, tiled=True)
     branch = lax.psum(branch, "trow").astype(jnp.float32)

time: 360 us -> 346 us (0.961)
  waiting for transfers between devices: 276 us -> 240 us
  starting transfers between devices: 0.54 us -> 18.4 us
    ppermute x0 -> x3, waiting for transfers between devices: none -> 47.2 us  [the longest x2 30.7 us: local(): lower.append(lax.ppermute(lower[-1] if lower else x, 'tcol', pairs))]
    all_gather x1, waiting for transfers between devices: 44.4 us -> 0.02 us  [local(): lax.all_gather(gelu_value(pre).astype(jnp.bfloat16), 'tcol', axis=0, tile...]
    all_gather x1 -> x0, waiting for transfers between devices: 40.3 us -> none  [local(): lax.all_gather((dhid * gelu_slope(pre)).astype(jnp.bfloat16), 'tcol', axi...]
    ppermute x0 -> x3, starting transfers between devices: none -> 17.9 us  [the longest x2 14.8 us: local(): lower.append(lax.ppermute(lower[-1] if lower else x, 'tcol', pairs))]
    reduce_scatter x1, waiting for transfers between devices: 15.6 us -> 23.2 us  [local(): lax.psum_scatter(branch_part, 'fsdp', scatter_dimension=0, tiled=True)]
    reduce_scatter x1, waiting for transfers between devices: 23.2 us -> 17.9 us  [local(): lax.psum_scatter(dnorm_part, 'fsdp', scatter_dimension=0, tiled=True)]
  transfers between devices with their start and end apart: 9 -> 11, of which waited for: 9 -> 10; matrix products, arithmetic and copies ran while one was open for 9% -> 11% of each run, Pallas kernels for 0% -> 0%
where the time goes in v1:
time: 346 us
  waiting for transfers between devices  240 us (69%)
  matrix products  33.5 us (10%)
  blocking collectives  25.2 us (7%)
  starting transfers between devices  18.4 us (5%)
  between operations  14.2 us (4%)
  other arithmetic  11.4 us (3%)
    reduce_scatter x1, waiting for transfers between devices, local(): lax.psum_scatter(dhid_part, 'tcol', scatter_dimension=0, tiled=True)  45.6 us
    reduce_scatter x1, waiting for transfers between devices, local(): lax.psum_scatter(pre_part, 'tcol', scatter_dimension=0, tiled=True)  40.3 us
    dot_general x6, matrix products, contract(): lax.dot_general(left, right, (((left_dim,), (right_dim,)), ((), ())), pre...  33.5 us
    ppermute x2, waiting for transfers between devices, local(): lower.append(lax.ppermute(lower[-1] if lower else x, 'tcol', pairs))  30.7 us
    psum x1, waiting for transfers between devices, local(): branch = lax.psum(branch, 'trow').astype(jnp.float32)  29.9 us
    reduce_scatter x1, waiting for transfers between devices, local(): lax.psum_scatter(branch_part, 'fsdp', scatter_dimension=0, tiled=True)  23.2 us
    all_gather x1, waiting for transfers between devices, local(): normed_all = lax.all_gather(normalized_rows, 'fsdp', axis=0, tiled=True)  18.9 us
    reduce_scatter x1, waiting for transfers between devices, local(): lax.psum_scatter(dnorm_part, 'fsdp', scatter_dimension=0, tiled=True)  17.9 us
  transfers between devices with their start and end apart: 11, of which 10 were waited for; matrix products, arithmetic and copies ran while one was open for 11% of the time, Pallas kernels for 0%

profile of v1, /device:TPU:0, one launch (start us, length us, event | category | flops | bytes accessed | tf_op | source)
XLA Modules:
  0.0 345.9 jit_solution(4506160823717079744)
XLA Ops:
  7.2 0.0 all-gather.4.cloned.1.call-start
  7.2 1.3 convert_reduce_fusion
  8.5 13.5 %all-reduce.1 = (f32[256]{0:T(256)S(1)}, f32[256]{0:T(256)S(1)}) all-reduce(f32[256]{0:T(256)S(1)} %get-tuple-element.7, f32[256]{0:T(256)S(1)} %get-tuple-element.6), channel_id=1, replica_groups=mesh['fsdp'=2,'trow'=4,'tcol'=4] {'tcol'}, use_global_device_ids=true, to_apply=%region_3.0 | all-reduce | flops 512 | bytes 4096 | tf_op jit(solution)/shard_map/psum | solution.py:33
  22.0 2.1 fusion.7
  24.1 0.0 all-gather.4.cloned.1.call-update
  24.1 0.0 all-gather.8.cloned.1.call-start
  24.2 0.7 all-gather.8.cloned.1.call-update
  24.9 0.0 reduce-scatter.5.cloned.1.call-start
  24.9 18.9 %all-gather.4.cloned.1.call-done = bf16[512,1024]{1,0:T(8,128)(2,1)} async-done(((bf16[256,1024]{1,0:T(8,128)(2,1)}), bf16[512,1024]{1,0:T(8,128)(2,1)}) %all-gather.4.cloned.1.call-update) | async-done | bytes 1048592 | tf_op jit(solution)/shard_map/all_gather | solution.py:41
  43.8 6.2 %convolution_convert_fusion.3 = bf16[512,2048]{1,0:T(8,128)(2,1)} fusion(bf16[512,1024]{1,0:T(8,128)(2,1)} %all-gather.4.cloned.1.call-done, bf16[1024,2048]{1,0:T(8,128)(2,1)} %param.5), kind=kOutput, calls=%fused_computation.4 | convolution fusion | flops 2148532224 | bytes 7340032 | tf_op jit(solution)/shard_map/dot_general | solution.py:24
  49.9 0.0 reduce-scatter.5.cloned.1.call-update
  49.9 0.0 reduce-scatter.9.cloned.1.call-start
  50.0 16.6 %all-gather.8.cloned.1.call-done = bf16[512,1024]{1,0:T(8,128)(2,1)} async-done(((bf16[256,1024]{1,0:T(8,128)(2,1)}), bf16[512,1024]{1,0:T(8,128)(2,1)}) %all-gather.8.cloned.1.call-update) | async-done | bytes 1048592 | tf_op jit(solution)/shard_map/all_gather | solution.py:32
  66.6 6.2 %convolution_convert_fusion.2 = bf16[512,2048]{1,0:T(8,128)(2,1)} fusion(bf16[512,1024]{1,0:T(8,128)(2,1)} %all-gather.8.cloned.1.call-done, bf16[2048,1024]{1,0:T(8,128)(2,1)} %param.6), kind=kOutput, calls=%fused_computation.3 | convolution fusion | flops 2148532224 | bytes 7340032 | tf_op jit(solution)/shard_map/dot_general | solution.py:24
  72.8 0.0 reduce-scatter.9.cloned.1.call-update
  72.8 0.0 all-gather.6.cloned.1.call-start
  72.9 40.3 %reduce-scatter.5.cloned.1.call-done = bf16[128,2048]{1,0:T(8,128)(2,1)} async-done(((bf16[512,2048]{1,0:T(8,128)(2,1)}), bf16[128,2048]{1,0:T(8,128)(2,1)}) %reduce-scatter.5.cloned.1.call-update) | async-done | bytes 524304 | tf_op jit(solution)/shard_map/reduce_scatter | solution.py:45
  113.2 45.6 %reduce-scatter.9.cloned.1.call-done = bf16[128,2048]{1,0:T(8,128)(2,1)} async-done(((bf16[512,2048]{1,0:T(8,128)(2,1)}), bf16[128,2048]{1,0:T(8,128)(2,1)}) %reduce-scatter.9.cloned.1.call-update) | async-done | bytes 524304 | tf_op jit(solution)/shard_map/reduce_scatter | solution.py:43
  158.7 2.5 fusion.18
  161.3 0.0 all-gather.6.cloned.1.call-update
  161.3 0.0 reduce-scatter.11.cloned.1.call-start
  161.3 0.7 collective-permute-start
  162.1 3.2 collective-permute-start.2
  165.2 17.8 %collective-permute-done = bf16[128,2048]{1,0:T(8,128)(2,1)S(1)} collective-permute-done((bf16[128,2048]{1,0:T(8,128)(2,1)S(1)}, bf16[128,2048]{1,0:T(8,128)(2,1)S(1)}, u32[]{:S(2)}, u32[]{:S(2)}) %collective-permute-start) | collective-permute-done | bytes 524320 | tf_op jit(solution)/shard_map/ppermute | solution.py:54
  183.0 14.1 %collective-permute-start.1 = (bf16[128,2048]{1,0:T(8,128)(2,1)S(1)}, bf16[128,2048]{1,0:T(8,128)(2,1)S(1)}, u32[]{:S(2)}, u32[]{:S(2)}) collective-permute-start(bf16[128,2048]{1,0:T(8,128)(2,1)S(1)} %collective-permute-done), channel_id=1, source_target_pairs={{0,1},{1,2},{2,3},{3,0},{4,5},{5,6},{6,7},{7,4},{8,9},{9,10},{10,1... | collective-permute-start | bytes 1572872 | tf_op jit(solution)/shard_map/ppermute | solution.py:54
  197.1 16.6 %collective-permute-done.2 = bf16[128,2048]{1,0:T(8,128)(2,1)S(1)} collective-permute-done((bf16[128,2048]{1,0:T(8,128)(2,1)S(1)}, bf16[128,2048]{1,0:T(8,128)(2,1)S(1)}, u32[]{:S(2)}, u32[]{:S(2)}) %collective-permute-start.2) | collective-permute-done | bytes 524320 | tf_op jit(solution)/shard_map/ppermute | solution.py:56
  213.7 0.0 copy-start.3
  213.7 12.8 %collective-permute-done.1 = bf16[128,2048]{1,0:T(8,128)(2,1)S(1)} collective-permute-done((bf16[128,2048]{1,0:T(8,128)(2,1)S(1)}, bf16[128,2048]{1,0:T(8,128)(2,1)S(1)}, u32[]{:S(2)}, u32[]{:S(2)}) %collective-permute-start.1) | collective-permute-done | bytes 524320 | tf_op jit(solution)/shard_map/ppermute | solution.py:54
  226.5 0.0 copy-start.4
  226.5 0.0 copy-done.3
  226.5 0.8 copy-done.4
  227.3 1.5 pad_maximum_fusion
  228.8 2.0 gather_fusion
  230.8 6.2 %convolution_convert_fusion.4 = bf16[512,1024]{1,0:T(8,128)(2,1)} fusion(bf16[512,2048]{1,0:T(8,128)(2,1)} %bitcast.19, bf16[1024,2048]{1,0:T(8,128)(2,1)} %param.5), kind=kOutput, calls=%fused_computation.18 | convolution fusion | flops 2148007936 | bytes 7340032 | tf_op jit(solution)/shard_map/dot_general | solution.py:24
  236.9 0.0 reduce-scatter.11.cloned.1.call-update
  236.9 0.0 reduce-scatter.7.cloned.1.call-start
  237.0 0.0 all-gather.6.cloned.1.call-done
  237.0 0.0 copy-start.6
  237.0 6.2 %convolution_convert_fusion.5 = bf16[512,1024]{1,0:T(8,128)(2,1)} fusion(bf16[512,2048]{1,0:T(8,128)(2,1)} %all-gather.6.cloned.1.call-done, bf16[2048,1024]{1,0:T(8,128)(2,1)} %param.6), kind=kOutput, calls=%fused_computation.19 | convolution fusion | flops 2148007936 | bytes 7340032 | tf_op jit(solution)/shard_map/dot_general | solution.py:24
  243.2 0.0 copy-start.1
  243.2 0.0 reduce-scatter.7.cloned.1.call-update
  243.3 0.2 all-reduce.5.cloned.1.call-start
  243.5 17.9 %reduce-scatter.11.cloned.1.call-done = bf16[256,1024]{1,0:T(8,128)(2,1)} async-done(((bf16[512,1024]{1,0:T(8,128)(2,1)}), bf16[256,1024]{1,0:T(8,128)(2,1)}) %reduce-scatter.11.cloned.1.call-update) | async-done | bytes 524304 | tf_op jit(solution)/shard_map/reduce_scatter | solution.py:67
  261.4 23.2 %reduce-scatter.7.cloned.1.call-done = bf16[256,1024]{1,0:T(8,128)(2,1)} async-done(((bf16[512,1024]{1,0:T(8,128)(2,1)}), bf16[256,1024]{1,0:T(8,128)(2,1)}) %reduce-scatter.7.cloned.1.call-update) | async-done | bytes 524304 | tf_op jit(solution)/shard_map/reduce_scatter | solution.py:62
  284.6 0.0 all-reduce.5.cloned.1.call-update
  284.6 0.0 copy-done.6
  284.6 0.0 copy-done.1
  284.6 0.0 copy-start.5
  284.7 0.0 copy-start.7
  284.7 4.4 %convolution_convert_fusion.1 = bf16[1024,2048]{1,0:T(8,128)(2,1)} fusion(bf16[512,1024]{1,0:T(8,128)(2,1)S(1)} %copy-done.6, bf16[512,2048]{1,0:T(8,128)(2,1)S(1)} %bitcast.20), kind=kOutput, calls=%fused_computation.2 | convolution fusion | flops 2149580800 | bytes 7340032 | tf_op jit(solution)/shard_map/dot_general | solution.py:24
  289.1 0.0 copy-done.5
  289.1 0.0 copy-done.7
  289.1 0.0 copy-start
  289.1 0.0 copy-start.2
  289.1 4.4 %convolution_convert_fusion = bf16[2048,1024]{1,0:T(8,128)(2,1)} fusion(bf16[512,2048]{1,0:T(8,128)(2,1)S(1)} %copy-done.5, bf16[512,1024]{1,0:T(8,128)(2,1)S(1)} %copy-done.7), kind=kOutput, calls=%fused_computation.1 | convolution fusion | flops 2149580800 | bytes 7340032 | tf_op jit(solution)/shard_map/dot_general | solution.py:24
  293.5 29.9 %all-reduce.5.cloned.1.call-done = (bf16[256,1024]{1,0:T(8,128)(2,1)}, bf16[256,1024]{1,0:T(8,128)(2,1)}) async-done(((bf16[256,1024]{1,0:T(8,128)(2,1)}, bf16[256,1024]{1,0:T(8,128)(2,1)}), (bf16[256,1024]{1,0:T(8,128)(2,1)}, bf16[256,1024]{1,0:T(8,128)(2,1)})) %all-reduce.5.cloned.1.call-update) | async-done | bytes 1048592 | tf_op jit(solution)/shard_map/psum | solution.py:63
  323.4 0.0 copy-done
  323.4 1.5 convert_reduce_fusion.1
  324.8 11.7 %all-reduce = (f32[256]{0:T(256)S(1)}, f32[256]{0:T(256)S(1)}) all-reduce(f32[256]{0:T(256)S(1)} %get-tuple-element.5, f32[256]{0:T(256)S(1)} %get-tuple-element.4), channel_id=1, replica_groups=mesh['fsdp'=2,'trow'=4,'tcol'=4] {'tcol'}, use_global_device_ids=true, to_apply=%region_13.14 | all-reduce | flops 512 | bytes 4096 | tf_op jit(solution)/shard_map/psum | solution.py:70
  336.5 0.0 copy-done.2
  336.5 2.6 fusion.3
  (4 shorter events, 0.0 us)
Async XLA Ops:
  7.2 36.6 %all-gather.4.cloned.1.call-start = ((), (), s32[]{:S(2)}) async-start(), calls=%async_computation.4 | async-start | bytes 1572864 | tf_op jit(solution)/shard_map/all_gather | solution.py:41
  24.1 42.5 %all-gather.8.cloned.1.call-start = ((), (), s32[]{:S(2)}) async-start(), calls=%async_computation.8 | async-start | bytes 1572864 | tf_op jit(solution)/shard_map/all_gather | solution.py:32
  24.9 88.3 %reduce-scatter.5.cloned.1.call-start = ((), (), s32[]{:S(2)}) async-start(), calls=%async_computation.5 | async-start | bytes 2621440 | tf_op jit(solution)/shard_map/reduce_scatter | solution.py:45
  49.9 108.8 %reduce-scatter.9.cloned.1.call-start = ((), (), s32[]{:S(2)}) async-start(), calls=%async_computation.9 | async-start | bytes 2621440 | tf_op jit(solution)/shard_map/reduce_scatter | solution.py:43
  72.8 164.2 %all-gather.6.cloned.1.call-start = ((), (), s32[]{:S(2)}) async-start(), calls=%async_computation.6 | async-start | bytes 2621440 | tf_op jit(solution)/shard_map/all_gather | solution.py:46
  161.3 100.1 %reduce-scatter.11.cloned.1.call-start = ((), (), s32[]{:S(2)}) async-start(), calls=%async_computation.10 | async-start | bytes 1572864 | tf_op jit(solution)/shard_map/reduce_scatter | solution.py:67
  161.3 21.7 %collective-permute-start = (bf16[128,2048]{1,0:T(8,128)(2,1)S(1)}, bf16[128,2048]{1,0:T(8,128)(2,1)S(1)}, u32[]{:S(2)}, u32[]{:S(2)}) collective-permute-start(bf16[128,2048]{1,0:T(8,128)(2,1)S(1)} %get-tuple-element.16), channel_id=1, source_target_pairs={{0,1},{1,2},{2,3},{3,0},{4,5},{5,6},{6,7},{7,4},{8,9},{9,10},{10,1... | collective-permute-start | bytes 1572872 | tf_op jit(solution)/shard_map/ppermute | solution.py:54
  162.1 51.6 %collective-permute-start.2 = (bf16[128,2048]{1,0:T(8,128)(2,1)S(1)}, bf16[128,2048]{1,0:T(8,128)(2,1)S(1)}, u32[]{:S(2)}, u32[]{:S(2)}) collective-permute-start(bf16[128,2048]{1,0:T(8,128)(2,1)S(1)} %get-tuple-element.16), channel_id=1, source_target_pairs={{1,0},{2,1},{3,2},{0,3},{5,4},{6,5},{7,6},{4,7},{9,8},{10,9},{11,1... | collective-permute-start | bytes 1572872 | tf_op jit(solution)/shard_map/ppermute | solution.py:56
  183.0 43.5 %collective-permute-start.1 = (bf16[128,2048]{1,0:T(8,128)(2,1)S(1)}, bf16[128,2048]{1,0:T(8,128)(2,1)S(1)}, u32[]{:S(2)}, u32[]{:S(2)}) collective-permute-start(bf16[128,2048]{1,0:T(8,128)(2,1)S(1)} %collective-permute-done), channel_id=1, source_target_pairs={{0,1},{1,2},{2,3},{3,0},{4,5},{5,6},{6,7},{7,4},{8,9},{9,10},{10,1... | collective-permute-start | bytes 1572872 | tf_op jit(solution)/shard_map/ppermute | solution.py:54
  213.7 12.8 %copy-start.3 = (bf16[128,2048]{1,0:T(8,128)(2,1)}, bf16[128,2048]{1,0:T(8,128)(2,1)S(1)}, u32[]{:S(2)}) copy-start(bf16[128,2048]{1,0:T(8,128)(2,1)S(1)} %collective-permute-done.2) | copy-start | bytes 1572868
  226.5 0.8 copy-start.4
  236.9 47.7 %reduce-scatter.7.cloned.1.call-start = ((), (), s32[]{:S(2)}) async-start(), calls=%async_computation.7 | async-start | bytes 1572864 | tf_op jit(solution)/shard_map/reduce_scatter | solution.py:62
  237.0 47.6 %copy-start.6 = (bf16[512,1024]{1,0:T(8,128)(2,1)S(1)}, bf16[512,1024]{1,0:T(8,128)(2,1)}, u32[]{:S(2)}) copy-start(bf16[512,1024]{1,0:T(8,128)(2,1)} %all-gather.4.cloned.1.call-done) | copy-start | bytes 3145732
  243.2 41.4 %copy-start.1 = (bf16[4,128,2048]{2,1,0:T(8,128)(2,1)S(1)}, bf16[4,128,2048]{2,1,0:T(8,128)(2,1)}, u32[]{:S(2)}) copy-start(bf16[4,128,2048]{2,1,0:T(8,128)(2,1)} %gather_fusion) | copy-start | bytes 6291460
  243.3 80.1 %all-reduce.5.cloned.1.call-start = ((), (), s32[]{:S(2)}) async-start(), calls=%async_computation.11 | async-start | bytes 2097152 | tf_op jit(solution)/shard_map/psum | solution.py:63
  284.6 4.4 %copy-start.5 = (bf16[512,2048]{1,0:T(8,128)(2,1)S(1)}, bf16[512,2048]{1,0:T(8,128)(2,1)}, u32[]{:S(2)}) copy-start(bf16[512,2048]{1,0:T(8,128)(2,1)} %all-gather.6.cloned.1.call-done) | copy-start | bytes 6291460
  284.7 4.4 %copy-start.7 = (bf16[512,1024]{1,0:T(8,128)(2,1)S(1)}, bf16[512,1024]{1,0:T(8,128)(2,1)}, u32[]{:S(2)}) copy-start(bf16[512,1024]{1,0:T(8,128)(2,1)} %all-gather.8.cloned.1.call-done) | copy-start | bytes 3145732
  289.1 34.3 %copy-start = (bf16[256,1024]{1,0:T(8,128)(2,1)S(1)}, bf16[256,1024]{1,0:T(8,128)(2,1)}, u32[]{:S(2)}) copy-start(bf16[256,1024]{1,0:T(8,128)(2,1)} %param.4) | copy-start | bytes 1572868
  289.1 47.5 %copy-start.2 = (bf16[256,1024]{1,0:T(8,128)(2,1)S(1)}, bf16[256,1024]{1,0:T(8,128)(2,1)}, u32[]{:S(2)}) copy-start(bf16[256,1024]{1,0:T(8,128)(2,1)} %param.7) | copy-start | bytes 1572868
Sparse Core Ops, SparseCore 0:
  24.2 19.4 all-gather.3
  45.3 21.2 all-gather.7
  69.5 43.6 reduce-scatter.4
  115.9 42.8 reduce-scatter.8
  161.4 71.4 all-gather.5
  237.1 24.2 reduce-scatter.10
  264.2 20.3 reduce-scatter.6
  287.0 36.2 all-reduce.4
